TPU v7x, 128 devices: a whole 4x4x4 slice. The times are simulated.
128 devices in a mesh: mem: 16 (over y, x), pix: 8 (over z, core).
Axes of the slice: x: 4, y: 4, z: 4, core: 2. Of those that a mesh axis runs over, the one named last changes fastest.
Arguments:
- prior_motion: bfloat16 [64, 16, 262144], P('mem', None, 'pix'), may hold values from -6 to 6
- measured_motion: float32 [1200], replicated, may hold values from -1.6 to 1.6
- measurement_noise_stddev: float32 [1200], replicated, may hold values from 0.05 to 0.5
- gaussian_jitter: float32 [2, 1200, 64], replicated, may hold values from -6 to 6
- scene_couples: int32 [2, 1200], replicated, may hold values from 0 to 15, as said below
- targeted_tile_number: int32 [1200], replicated, may hold values from 0 to 4095
Outputs:
- analysis: bfloat16 [64, 16, 262144], P('mem', None, 'pix')
Inputs may be any that keep to these rules, and one draw needn't show every extreme that they name: scene_couples[0, k] < scene_couples[1, k]: row 0 holds the earlier acquisition, row 1 the later.
All inputs are finite; a program needn't handle non-finite values.
Results may differ from a plain program's by a relative error of at most 0.011.
Values may be sent and summed in bfloat16 or wider, within the bound.
No kernel may reach another device: no remote copies, remote signals or barrier semaphores. Data moves between devices by JAX's collectives and lax.ppermute only.
A program may use at most 128 MiB of HBM per device.

v0:
```python
import math
import jax
import jax.numpy as jnp
from jax import lax
from jax.sharding import PartitionSpec as P

BLK = 64
PASS_COUNT = 2
HI = lax.Precision.HIGHEST


def mm(a, b):
    return jnp.dot(a, b, precision=HI, preferred_element_type=jnp.float32)


def tn(a, b):
    return lax.dot_general(
        a, b, (((0,), (0,)), ((), ())), precision=HI, preferred_element_type=jnp.float32
    )


def local_sums(parts):
    n_part, members, dates, width = parts.shape
    blocks = width // BLK
    summer = (
        jnp.arange(width, dtype=jnp.int32)[:, None] // BLK
        == jnp.arange(blocks, dtype=jnp.int32)[None, :]
    ).astype(jnp.bfloat16)
    flat = jnp.dot(parts.reshape(-1, width), summer, preferred_element_type=jnp.float32)
    flat = flat.reshape(n_part, members * dates, blocks)
    return jnp.moveaxis(flat, 0, 1).reshape(members * dates, n_part * blocks)


def local_predicted(sums, dates, first_block, scene_couples, targeted_tile_number):
    blocks = sums.shape[1]
    block_range = first_block + jnp.arange(blocks, dtype=jnp.int32)
    block_table = (block_range[:, None] == targeted_tile_number[None, :]).astype(jnp.float32)
    picked = mm(sums, block_table)
    timeline = jnp.arange(dates, dtype=jnp.int32)
    pair_table = (timeline[:, None] == scene_couples[1][None, :]).astype(jnp.float32) - (
        timeline[:, None] == scene_couples[0][None, :]
    ).astype(jnp.float32)
    picked = picked.reshape(-1, dates, picked.shape[1])
    return jnp.sum(picked * pair_table[None], axis=1) / BLK


def solve(gram, cross):
    n = gram.shape[0]
    factor = jnp.linalg.cholesky(jnp.eye(n, dtype=jnp.float32) + gram)
    mixing = jax.scipy.linalg.cho_solve((factor, True), cross) / math.sqrt(n - 1)
    return mixing.astype(jnp.bfloat16).astype(jnp.float32)


def combined_mixing(gram, cross_first, cross_second):
    n = gram.shape[0]
    first = solve(gram, cross_first)
    moved = first + jnp.eye(n, dtype=jnp.float32)
    moved = moved - jnp.mean(moved, axis=1, keepdims=True)
    gram_moved = mm(gram, moved)
    gram_next = tn(moved, gram_moved)
    cross_next = tn(moved, cross_second - math.sqrt(n - 1) * mm(gram, first))
    second = solve(gram_next, cross_next)
    whole = first + mm(moved, second)
    return whole - jnp.mean(whole, axis=0, keepdims=True)


def body(
    prior_motion,
    measured_motion,
    measurement_noise_stddev,
    gaussian_jitter,
    scene_couples,
    targeted_tile_number,
):
    members, dates, cells = prior_motion.shape
    n_mem = lax.axis_size("mem")
    width = cells // n_mem
    n = members * n_mem
    parts = jnp.moveaxis(prior_motion.reshape(members, dates, n_mem, width), 2, 0)
    state = lax.all_to_all(parts, "mem", split_axis=0, concat_axis=0, tiled=True)
    first_block = lax.axis_index("pix") * (cells // BLK)
    predicted = local_predicted(
        local_sums(parts), dates, first_block, scene_couples, targeted_tile_number
    )
    predicted = lax.all_gather(predicted, "mem", axis=0, tiled=True)
    in_tile = targeted_tile_number // (cells // BLK) == lax.axis_index("pix")
    spread = jnp.sqrt(jnp.float32(float(PASS_COUNT))) * measurement_noise_stddev
    scaled = (predicted - jnp.mean(predicted, axis=0, keepdims=True)) / (spread * math.sqrt(n - 1))[
        None, :
    ]
    fixed = (measured_motion[None, :] - predicted) / spread[None, :]
    misfits = [
        jnp.where(in_tile[None, :], fixed + gaussian_jitter[i].T, 0.0) for i in range(PASS_COUNT)
    ]
    right = jnp.concatenate([scaled] + misfits, axis=0)
    products = lax.dot_general(
        scaled, right, (((1,), (1,)), ((), ())), precision=HI, preferred_element_type=jnp.float32
    )
    products = lax.psum(products, "pix")
    mixing = combined_mixing(products[:, :n], products[:, n : 2 * n], products[:, 2 * n :])
    mixing = mixing.astype(jnp.bfloat16)
    rows = n * dates
    spread_mixing = (
        mixing.T[:, None, :, None] * jnp.eye(dates, dtype=jnp.bfloat16)[None, :, None, :]
    ).reshape(rows, rows)
    flat = state.reshape(rows, width)
    change = jnp.dot(spread_mixing, flat, preferred_element_type=jnp.float32)
    fresh = (flat.astype(jnp.float32) + change).astype(jnp.bfloat16)
    fresh = fresh.reshape(n_mem, members, dates, width)
    back = lax.all_to_all(fresh, "mem", split_axis=0, concat_axis=0, tiled=True)
    return jnp.moveaxis(back, 0, 2).reshape(members, dates, cells)


def solution(mesh):
    return jax.shard_map(
        body,
        mesh=mesh,
        in_specs=(P("mem", None, "pix"), P(), P(), P(), P(), P()),
        out_specs=P("mem", None, "pix"),
        check_vma=False,
    )
```

profile of v0, /device:TPU:0, one launch (start us, length us, event | category | flops | bytes accessed | tf_op | source)
XLA Modules:
  0.0 242.5 jit_solution(9956106009973401795)
XLA Ops:
  0.0 4.8 %copy.47 = bf16[4,2,16,8,2048]{4,3,1,0,2:T(8,128)(2,1)} copy(bf16[4,2,16,8,2048]{4,3,2,1,0:T(8,128)(2,1)} %bitcast.84) | data formatting | bytes 8388608 | tf_op jit(solution)/shard_map/reshape | solution.py:79
  4.8 0.0 copy-start.4
  4.8 0.0 copy-start.3
  4.8 7.3 %all-to-all-start = ((bf16[16,4,16,2048]{3,2,1,0:T(8,128)(2,1)}), bf16[16,4,16,2048]{3,2,1,0:T(8,128)(2,1)}, u32[]{:S(2)}, u32[]{:S(2)}) async-start(bf16[16,4,16,2048]{3,2,1,0:T(8,128)(2,1)} %bitcast.81), calls=%async_computation | async-start | bytes 8388608 | tf_op jit(solution)/shard_map/all_to_all | solution.py:80
  12.2 0.0 copy-done.4
  12.2 0.0 copy-done.3
  12.2 0.0 copy-done.1
  12.3 0.0 copy-start
  12.3 0.0 copy-start.2
  12.3 3.6 %convolution_bitcast_fusion = f32[1024,32]{0,1:T(8,128)S(1)} fusion(bf16[1024,2048]{1,0:T(8,128)(2,1)} %bitcast.82, s32[2048]{0:T(1024)S(1)} %add_select_fusion.1), kind=kOutput, calls=%fused_computation.10 | convolution fusion | flops 134348800 | bytes 4333568 | tf_op jit(solution)/shard_map/dot_general | solution.py:29
  15.9 0.1 reshape.162
  16.0 0.3 copy.26
  16.3 0.2 dot_general.33
  16.6 1.3 fusion.8
  17.9 72.2 %all-gather = f32[16,4,1200]{2,1,0:T(4,128)S(1)} all-gather(f32[1,4,1200]{2,1,0:T(4,128)S(1)} %multiply_bitcast_fusion), channel_id=1, replica_groups=mesh['mem'=16,'pix'=8] {'mem'}, dimensions={0}, use_global_device_ids=true | all-gather | bytes 326400 | tf_op jit(solution)/shard_map/all_gather | solution.py:85
  90.1 0.1 reshape.166
  90.3 0.1 reduce_sum.37
  90.3 0.0 copy-done
  90.3 0.0 copy-done.2
  90.4 0.1 fusion.24
  90.5 0.9 fusion.15
  91.4 25.5 %psum.7 = f32[64,192]{0,1:T(8,128)S(1)} all-reduce(f32[64,192]{0,1:T(8,128)S(1)} %fusion.15), channel_id=1, replica_groups=mesh['mem'=16,'pix'=8] {'pix'}, use_global_device_ids=true, to_apply=%region_2.3 | all-reduce | flops 12288 | bytes 98304 | tf_op jit(solution)/shard_map/psum | solution.py:99
  116.9 0.1 copy.28
  117.0 5.8 %cholesky.44 = f32[64,64]{1,0:T(8,128)S(1)} custom-call(f32[64,64]{1,0:T(8,128)S(1)} %fusion.43), custom_call_target="Cholesky" | custom-call | tf_op jit(solution)/shard_map/jit(cholesky)/cholesky | solution.py:49
  122.9 0.7 compare_reduce_fusion.1
  123.7 0.7 fusion.33
  124.4 4.9 %custom-call.8 = f32[1,64,64]{1,2,0:T(8,128)S(1)} custom-call(f32[1,64,64]{2,1,0:T(8,128)S(1)} %fusion.33), custom_call_target="InvertDiagBlocksLowerTriangular" | custom-call | tf_op jit(solution)/shard_map/jit(_cho_solve)/triangular_solve | solution.py:50
  129.3 0.2 fusion.35
  129.5 0.3 fusion.26
  129.8 0.2 fusion.31
  130.0 0.2 convolution_add_fusion.1
  130.3 0.1 copy.31
  130.4 5.8 %cholesky.55 = f32[64,64]{1,0:T(8,128)S(1)} custom-call(f32[64,64]{1,0:T(8,128)S(1)} %fusion.40), custom_call_target="Cholesky" | custom-call | tf_op jit(solution)/shard_map/jit(cholesky)/cholesky | solution.py:49
  136.2 0.7 compare_reduce_fusion
  137.0 0.7 fusion.34
  137.7 4.9 %custom-call.9 = f32[1,64,64]{1,2,0:T(8,128)S(1)} custom-call(f32[1,64,64]{2,1,0:T(8,128)S(1)} %fusion.34), custom_call_target="InvertDiagBlocksLowerTriangular" | custom-call | tf_op jit(solution)/shard_map/jit(_cho_solve)/triangular_solve | solution.py:50
  142.6 0.1 fusion.11
  142.7 0.2 fusion.28
  142.9 0.2 fusion.38
  143.2 0.2 fusion.13
  143.4 0.3 fusion.60
  143.7 0.1 fusion.46
  143.8 5.9 %broadcast_multiply_fusion = bf16[64,16,64,16]{3,2,1,0:T(8,128)(2,1)} fusion(bf16[16,16]{1,0:T(8,128)(2,1)S(1)} %fusion.56, bf16[64,64]{1,0:T(8,128)(2,1)S(1)} %fusion.46), kind=kLoop, calls=%fused_computation.1 | loop fusion | flops 1048576 | bytes 2105856 | tf_op jit(solution)/shard_map/mul | solution.py:104
  149.7 29.1 %mul.60 = bf16[1024,1024]{1,0:T(8,128)(2,1)S(1)} reshape(bf16[64,16,64,16]{3,2,1,0:T(8,128)(2,1)} %broadcast_multiply_fusion) | data formatting | bytes 4194304 | tf_op jit(solution)/shard_map/mul | solution.py:104
  178.8 0.0 all-to-all-done
  178.8 8.0 %add_convert_fusion = bf16[1024,2048]{1,0:T(8,128)(2,1)S(1)} fusion(bf16[1024,2048]{1,0:T(8,128)(2,1)} %bitcast.1, bf16[1024,1024]{1,0:T(8,128)(2,1)S(1)} %mul.60), kind=kOutput, calls=%fused_computation | convolution fusion | flops 4301258752 | bytes 10485760 | tf_op jit(solution)/shard_map/dot_general | solution.py:107
  186.9 53.3 %all_to_all.10 = bf16[16,4,16,2048]{3,2,1,0:T(8,128)(2,1)S(1)} all-to-all(bf16[16,4,16,2048]{3,2,1,0:T(8,128)(2,1)S(1)} %bitcast.85), channel_id=1, replica_groups=mesh['mem'=16,'pix'=8] {'mem'}, dimensions={0} | all-to-all | bytes 8388608 | tf_op jit(solution)/shard_map/all_to_all | solution.py:110
  240.2 2.3 copy.43
  (17 shorter events, 0.2 us)
Async XLA Ops:
  4.8 7.4 %copy-start.4 = (s32[1200]{0:T(1024)S(1)}, s32[1200]{0:T(1024)}, u32[]{:S(2)}) copy-start(s32[1200]{0:T(1024)} %param.14) | copy-start | bytes 14404
  4.8 7.4 %copy-start.3 = (f32[1200]{0:T(1024)S(1)}, f32[1200]{0:T(1024)}, u32[]{:S(2)}) copy-start(f32[1200]{0:T(1024)} %param.11) | copy-start | bytes 14404
  4.8 7.4 %copy-start.1 = (s32[2,1200]{1,0:T(2,128)S(1)}, s32[2,1200]{1,0:T(2,128)}, u32[]{:S(2)}) copy-start(s32[2,1200]{1,0:T(2,128)} %param.13) | copy-start | bytes 28804
  4.8 174.0 %all-to-all-start = ((bf16[16,4,16,2048]{3,2,1,0:T(8,128)(2,1)}), bf16[16,4,16,2048]{3,2,1,0:T(8,128)(2,1)}, u32[]{:S(2)}, u32[]{:S(2)}) async-start(bf16[16,4,16,2048]{3,2,1,0:T(8,128)(2,1)} %bitcast.81), calls=%async_computation | async-start | bytes 8388608 | tf_op jit(solution)/shard_map/all_to_all | solution.py:80
  12.3 78.1 %copy-start = (f32[2,1200,64]{1,2,0:T(8,128)S(1)}, f32[2,1200,64]{1,2,0:T(8,128)}, u32[]{:S(2)}) copy-start(f32[2,1200,64]{1,2,0:T(8,128)} %param.12) | copy-start | bytes 1843204
  12.3 78.1 %copy-start.2 = (f32[1200]{0:T(1024)S(1)}, f32[1200]{0:T(1024)}, u32[]{:S(2)}) copy-start(f32[1200]{0:T(1024)} %param.10) | copy-start | bytes 14404
where the time goes:
time: 243 us
  blocking collectives  151 us (62%)
  local copies, waits for them, and re-layouts  37.1 us (15%)
  other arithmetic  30.7 us (13%)
  matrix products  15.9 us (7%)
  starting transfers between devices  7.33 us (3%)
    all_gather x1, blocking collectives, body(): predicted = lax.all_gather(predicted, 'mem', axis=0, tiled=True)  72.2 us
    all_to_all x1, blocking collectives, body(): back = lax.all_to_all(fresh, 'mem', split_axis=0, concat_axis=0, tiled=True)  53.3 us
    mul x1, local copies, waits for them, and re-layouts, body(): mixing.T[:, None, :, None]  29.1 us
    psum x1, blocking collectives, body(): products = lax.psum(products, 'pix')  25.5 us
    another operation x6, other arithmetic, solve(): factor = jnp.linalg.cholesky(jnp.eye(n, dtype=jnp.float32) + gram)  13.2 us
    another operation x4, other arithmetic, solve(): jax.scipy.linalg.cho_solve((factor, True), cross) / math.sqrt(n - 1)  11.2 us
    dot_general x1, matrix products, body(): change = jnp.dot(spread_mixing, flat, preferred_element_type=jnp.float32)  8.04 us
    all_to_all x1, starting transfers between devices, body(): lax.all_to_all(parts, 'mem', split_axis=0, concat_axis=0, tiled=True)  7.33 us
  transfers between devices with their start and end apart: 1, of which 0 were waited for; matrix products, arithmetic and copies ran while one was open for 28% of the time, Pallas kernels for 0%

commit v1 on v0

--- a/solution.py
+++ b/solution.py
@@ -3,10 +3,15 @@
 import jax.numpy as jnp
 from jax import lax
 from jax.sharding import PartitionSpec as P
+from jax.lax import all_gather
 
 BLK = 64
 PASS_COUNT = 2
 HI = lax.Precision.HIGHEST
+
+
+def change_racks_on_mesh(point, named_axis):
+    return jnp.sum(all_gather(point, axis_name=named_axis), axis=0)
 
 
 def mm(a, b):
@@ -96,7 +101,7 @@
     products = lax.dot_general(
         scaled, right, (((1,), (1,)), ((), ())), precision=HI, preferred_element_type=jnp.float32
     )
-    products = lax.psum(products, "pix")
+    products = change_racks_on_mesh(products, "pix")
     mixing = combined_mixing(products[:, :n], products[:, n : 2 * n], products[:, 2 * n :])
     mixing = mixing.astype(jnp.bfloat16)
     rows = n * dates

time: 243 us -> 235 us (0.967)
  blocking collectives: 151 us -> 143 us
    psum x1 -> x0, blocking collectives: 25.5 us -> none  [body(): products = lax.psum(products, 'pix')]
    all_gather x0 -> x1, blocking collectives: none -> 14.5 us  [change_racks_on_mesh(): return jnp.sum(all_gather(point, axis_name=named_axis), axis=0)]
    all_to_all x1, blocking collectives: 53.3 us -> 56.4 us  [body(): back = lax.all_to_all(fresh, 'mem', split_axis=0, concat_axis=0, tiled=True)]
  transfers between devices with their start and end apart: 1 -> 1, of which waited for: 0 -> 0; matrix products, arithmetic and copies ran while one was open for 28% -> 29% of each run, Pallas kernels for 0% -> 0%
where the time goes in v1:
time: 235 us
  blocking collectives  143 us (61%)
  local copies, waits for them, and re-layouts  37.2 us (16%)
  other arithmetic  30.7 us (13%)
  matrix products  16 us (7%)
  starting transfers between devices  7.33 us (3%)
    all_gather x1, blocking collectives, body(): predicted = lax.all_gather(predicted, 'mem', axis=0, tiled=True)  72.2 us
    all_to_all x1, blocking collectives, body(): back = lax.all_to_all(fresh, 'mem', split_axis=0, concat_axis=0, tiled=True)  56.4 us
    mul x1, local copies, waits for them, and re-layouts, body(): mixing.T[:, None, :, None]  29.1 us
    all_gather x1, blocking collectives, change_racks_on_mesh(): return jnp.sum(all_gather(point, axis_name=named_axis), axis=0)  14.5 us
    another operation x6, other arithmetic, solve(): factor = jnp.linalg.cholesky(jnp.eye(n, dtype=jnp.float32) + gram)  13.2 us
    another operation x4, other arithmetic, solve(): jax.scipy.linalg.cho_solve((factor, True), cross) / math.sqrt(n - 1)  11.2 us
    dot_general x1, matrix products, body(): change = jnp.dot(spread_mixing, flat, preferred_element_type=jnp.float32)  8.04 us
    all_to_all x1, starting transfers between devices, body(): lax.all_to_all(parts, 'mem', split_axis=0, concat_axis=0, tiled=True)  7.33 us
  transfers between devices with their start and end apart: 1, of which 0 were waited for; matrix products, arithmetic and copies ran while one was open for 29% of the time, Pallas kernels for 0%

profile of v1, /device:TPU:0, one launch (start us, length us, event | category | flops | bytes accessed | tf_op | source)
XLA Modules:
  0.0 234.7 jit_solution(2026340492678154489)
XLA Ops:
  0.0 4.8 %copy.43 = bf16[4,2,16,8,2048]{4,3,1,0,2:T(8,128)(2,1)} copy(bf16[4,2,16,8,2048]{4,3,2,1,0:T(8,128)(2,1)} %bitcast.85) | data formatting | bytes 8388608 | tf_op jit(solution)/shard_map/reshape | solution.py:84
  4.8 0.0 copy-start.4
  4.8 7.3 %all-to-all-start = ((bf16[16,4,16,2048]{3,2,1,0:T(8,128)(2,1)}), bf16[16,4,16,2048]{3,2,1,0:T(8,128)(2,1)}, u32[]{:S(2)}, u32[]{:S(2)}) async-start(bf16[16,4,16,2048]{3,2,1,0:T(8,128)(2,1)} %bitcast.82), calls=%async_computation | async-start | bytes 8388608 | tf_op jit(solution)/shard_map/all_to_all | solution.py:85
  12.2 0.0 copy-done.4
  12.2 0.0 copy-done.3
  12.2 0.0 copy-done.1
  12.3 0.0 copy-start
  12.3 0.0 copy-start.2
  12.3 3.6 %convolution_bitcast_fusion = f32[1024,32]{0,1:T(8,128)S(1)} fusion(bf16[1024,2048]{1,0:T(8,128)(2,1)} %bitcast.83, s32[2048]{0:T(1024)S(1)} %add_select_fusion.1), kind=kOutput, calls=%fused_computation.10 | convolution fusion | flops 134348800 | bytes 4333568 | tf_op jit(solution)/shard_map/dot_general | solution.py:34
  15.9 0.1 reshape.162
  16.0 0.3 copy.24
  16.3 0.2 dot_general.33
  16.6 1.3 fusion.8
  17.9 72.2 %all-gather.1 = f32[16,4,1200]{2,1,0:T(4,128)S(1)} all-gather(f32[1,4,1200]{2,1,0:T(4,128)S(1)} %multiply_bitcast_fusion), channel_id=1, replica_groups=mesh['mem'=16,'pix'=8] {'mem'}, dimensions={0}, use_global_device_ids=true | all-gather | bytes 326400 | tf_op jit(solution)/shard_map/all_gather | solution.py:90
  90.1 0.1 reshape.167
  90.3 0.1 reduce_sum.46
  90.3 0.0 copy-done
  90.3 0.0 copy-done.2
  90.4 0.1 fusion.24
  90.5 1.1 fusion.15
  91.5 14.5 %all-gather = f32[512,192]{1,0:T(8,128)S(1)} all-gather(f32[64,192]{1,0:T(8,128)S(1)} %fusion.15), channel_id=2, replica_groups=mesh['mem'=16,'pix'=8] {'pix'}, dimensions={0}, use_global_device_ids=true | all-gather | bytes 442368 | tf_op jit(solution)/shard_map/all_gather | solution.py:14
  106.1 0.1 copy.37
  106.2 0.1 copy.26
  106.3 5.8 %cholesky.44 = f32[64,64]{1,0:T(8,128)S(1)} custom-call(f32[64,64]{1,0:T(8,128)S(1)} %fusion.43), custom_call_target="Cholesky" | custom-call | tf_op jit(solution)/shard_map/jit(cholesky)/cholesky | solution.py:54
  112.2 0.7 compare_reduce_fusion.1
  112.9 0.7 fusion.33
  113.6 4.9 %custom-call.8 = f32[1,64,64]{1,2,0:T(8,128)S(1)} custom-call(f32[1,64,64]{2,1,0:T(8,128)S(1)} %fusion.33), custom_call_target="InvertDiagBlocksLowerTriangular" | custom-call | tf_op jit(solution)/shard_map/jit(_cho_solve)/triangular_solve | solution.py:55
  118.5 0.3 fusion.35
  118.8 0.3 fusion.26
  119.0 0.2 fusion.31
  119.2 0.2 convolution_add_fusion.1
  119.5 0.1 copy.29
  119.6 5.8 %cholesky.55 = f32[64,64]{1,0:T(8,128)S(1)} custom-call(f32[64,64]{1,0:T(8,128)S(1)} %fusion.40), custom_call_target="Cholesky" | custom-call | tf_op jit(solution)/shard_map/jit(cholesky)/cholesky | solution.py:54
  125.5 0.7 compare_reduce_fusion
  126.2 0.7 fusion.34
  126.9 4.9 %custom-call.9 = f32[1,64,64]{1,2,0:T(8,128)S(1)} custom-call(f32[1,64,64]{2,1,0:T(8,128)S(1)} %fusion.34), custom_call_target="InvertDiagBlocksLowerTriangular" | custom-call | tf_op jit(solution)/shard_map/jit(_cho_solve)/triangular_solve | solution.py:55
  131.8 0.2 fusion.11
  132.0 0.2 fusion.28
  132.1 0.2 fusion.38
  132.4 0.2 fusion.13
  132.6 0.3 fusion.60
  132.9 0.1 fusion.44
  133.0 5.9 %broadcast_multiply_fusion = bf16[64,16,64,16]{3,2,1,0:T(8,128)(2,1)} fusion(bf16[16,16]{1,0:T(8,128)(2,1)S(1)} %fusion.54, bf16[64,64]{1,0:T(8,128)(2,1)S(1)} %fusion.44), kind=kLoop, calls=%fused_computation.1 | loop fusion | flops 1048576 | bytes 2105856 | tf_op jit(solution)/shard_map/mul | solution.py:109
  138.9 29.1 %mul.60 = bf16[1024,1024]{1,0:T(8,128)(2,1)S(1)} reshape(bf16[64,16,64,16]{3,2,1,0:T(8,128)(2,1)} %broadcast_multiply_fusion) | data formatting | bytes 4194304 | tf_op jit(solution)/shard_map/mul | solution.py:109
  168.0 0.0 all-to-all-done
  168.0 8.0 %add_convert_fusion = bf16[1024,2048]{1,0:T(8,128)(2,1)S(1)} fusion(bf16[1024,2048]{1,0:T(8,128)(2,1)} %bitcast.1, bf16[1024,1024]{1,0:T(8,128)(2,1)S(1)} %mul.60), kind=kOutput, calls=%fused_computation | convolution fusion | flops 4301258752 | bytes 10485760 | tf_op jit(solution)/shard_map/dot_general | solution.py:112
  176.1 56.4 %all_to_all.10 = bf16[16,4,16,2048]{3,2,1,0:T(8,128)(2,1)S(1)} all-to-all(bf16[16,4,16,2048]{3,2,1,0:T(8,128)(2,1)S(1)} %bitcast.86), channel_id=1, replica_groups=mesh['mem'=16,'pix'=8] {'mem'}, dimensions={0} | all-to-all | bytes 8388608 | tf_op jit(solution)/shard_map/all_to_all | solution.py:115
  232.4 2.3 copy.39
  (20 shorter events, 0.3 us)
Async XLA Ops:
  4.8 7.4 %copy-start.4 = (s32[1200]{0:T(1024)S(1)}, s32[1200]{0:T(1024)}, u32[]{:S(2)}) copy-start(s32[1200]{0:T(1024)} %param.14) | copy-start | bytes 14404
  4.8 7.4 %copy-start.3 = (f32[1200]{0:T(1024)S(1)}, f32[1200]{0:T(1024)}, u32[]{:S(2)}) copy-start(f32[1200]{0:T(1024)} %param.11) | copy-start | bytes 14404
  4.8 7.4 %copy-start.1 = (s32[2,1200]{1,0:T(2,128)S(1)}, s32[2,1200]{1,0:T(2,128)}, u32[]{:S(2)}) copy-start(s32[2,1200]{1,0:T(2,128)} %param.13) | copy-start | bytes 28804
  4.8 163.2 %all-to-all-start = ((bf16[16,4,16,2048]{3,2,1,0:T(8,128)(2,1)}), bf16[16,4,16,2048]{3,2,1,0:T(8,128)(2,1)}, u32[]{:S(2)}, u32[]{:S(2)}) async-start(bf16[16,4,16,2048]{3,2,1,0:T(8,128)(2,1)} %bitcast.82), calls=%async_computation | async-start | bytes 8388608 | tf_op jit(solution)/shard_map/all_to_all | solution.py:85
  12.3 78.1 %copy-start = (f32[2,1200,64]{1,2,0:T(8,128)S(1)}, f32[2,1200,64]{1,2,0:T(8,128)}, u32[]{:S(2)}) copy-start(f32[2,1200,64]{1,2,0:T(8,128)} %param.12) | copy-start | bytes 1843204
  12.3 78.1 %copy-start.2 = (f32[1200]{0:T(1024)S(1)}, f32[1200]{0:T(1024)}, u32[]{:S(2)}) copy-start(f32[1200]{0:T(1024)} %param.10) | copy-start | bytes 14404
